TPU v7x, 32 devices: a whole 2x2x4 slice. The times are simulated.
32 devices in a mesh: groups: 2 (over y), cols: 4 (over z), rows: 4 (over x, core).
Axes of the slice: x: 2, y: 2, z: 4, core: 2. Of those that a mesh axis runs over, the one named last changes fastest.
Arguments:
- base_field: float32 [320, 64, 512], P(None, ('groups', 'cols'), 'rows'), parts along dimension 1, may hold values from -6 to 6
- control_field: float32 [320, 64, 512], P(None, ('groups', 'cols', 'rows')), parts along dimension 1, may hold values from -6 to 6
- first_kernel: bfloat16 [9, 320, 320], replicated, may hold values from -0.109375 to 0.109375
- second_kernel: bfloat16 [9, 320, 320], replicated, may hold values from -0.109375 to 0.109375
- control_kernel: bfloat16 [9, 320, 320], replicated, may hold values from -0.109375 to 0.109375
- first_bias: float32 [320], replicated, may hold values from -3 to 3
- second_bias: float32 [320], replicated, may hold values from -3 to 3
- control_bias: float32 [320], replicated, may hold values from -3 to 3
- to_control: bfloat16 [320, 320], replicated, may hold values from -0.3125 to 0.3125
- to_base: bfloat16 [320, 320], replicated, may hold values from -0.3125 to 0.3125
Outputs:
- base_out: float32 [320, 64, 512], P(None, ('groups', 'cols'), 'rows'), parts along dimension 1
- control_out: float32 [320, 64, 512], P(None, ('groups', 'cols', 'rows')), parts along dimension 1
There are 2 independent parts, one for each index of `groups`. A program takes and returns all parts, laid end to end along the dimension named above; an argument that names none is the same for every part. Nothing has to cross between parts.
All inputs are finite; a program needn't handle non-finite values.
Results may differ from a plain program's by a relative error of at most 0.0033.
Values may be sent and summed in bfloat16 or wider, within the bound.
A program may use at most 64 MiB of HBM per device.

v0:
```python
import functools

import jax
import jax.numpy as jnp
from jax import lax
from jax.experimental import pallas as pl
from jax.experimental.pallas import tpu as pltpu
from jax.sharding import PartitionSpec as P

MESH = pl.DeviceIdType.MESH
BF = jnp.bfloat16
F32 = jnp.float32
LANE = 128
PACK = 16
SIDES = ((-1, 0), (1, 0), (0, -1), (0, 1), (-1, -1), (1, -1), (-1, 1), (1, 1))


def silu(v):
    return 0.5 * v * (1.0 + jnp.tanh(0.5 * v))


def kernel(
    n_cols,
    n_rows,
    base_hbm,
    control_hbm,
    k1_hbm,
    k2_hbm,
    kc_hbm,
    b1_ref,
    b2_ref,
    bc_ref,
    tc_ref,
    tb_ref,
    base_out,
    control_out,
    base,
    control,
    raw,
    packed,
    shifts_b,
    shifts_h,
    shifts_c,
    biases,
    edge_out,
    edge_in,
    strips,
    mid,
    result,
    bracket,
    arrived,
    load_sem,
    x_send,
    x_recv,
    in_send,
    in_recv,
    out_send,
    out_recv,
):
    C = base.shape[0]
    tile_cols = base.shape[1]
    strip_cols = control.shape[1]
    wide = strip_cols * LANE
    main = C - C % LANE
    rest = C - main
    full = packed.shape[1] - C
    gid = lax.axis_index("groups")
    k = lax.axis_index("cols")
    r = lax.axis_index("rows")
    lane = lax.broadcasted_iota(jnp.int32, (C, LANE), 1)

    loads = []
    for i, (src, dst) in enumerate(
        (
            (base_hbm, base),
            (control_hbm, control),
            (k1_hbm, raw.at[0]),
            (k2_hbm, raw.at[1]),
            (kc_hbm, raw.at[2]),
        )
    ):
        copy = pltpu.make_async_copy(src, dst, load_sem.at[i])
        copy.start()
        loads.append(copy)

    def there(side):
        dk, dr = side
        ok = None
        for at, step, count in ((k, dk, n_cols), (r, dr, n_rows)):
            if step:
                test = (at > 0) if step < 0 else (at < count - 1)
                ok = test if ok is None else jnp.logical_and(ok, test)
        return ok

    def partner(o):
        if n_rows & (n_rows - 1):
            return lax.rem(r + o, n_rows), lax.rem(r + n_rows - o, n_rows)
        q, bit = r, 1
        while bit < n_rows:
            if o & bit:
                q = q + bit * (1 - 2 * lax.rem(lax.div(r, bit), 2))
            bit *= 2
        return q, q

    order = [o for o in range(n_rows // 2, n_rows)] + [o for o in range(1, n_rows // 2)]

    barrier = pltpu.get_barrier_semaphore()
    peers = n_rows - 1
    for side in SIDES:
        if side[0]:
            peers = peers + jnp.where(there(side), 1, 0)

            @pl.when(there(side))
            def _():
                pl.semaphore_signal(
                    barrier, inc=1, device_id=(gid, k + side[0], r + side[1]), device_id_type=MESH
                )
    for o in order:
        pl.semaphore_signal(barrier, inc=1, device_id=(gid, k, partner(o)[0]), device_id_type=MESH)

    def entered():
        pl.semaphore_wait(barrier, peers)

    def slot(s, count=1):
        return pl.ds(s * LANE, count * LANE)

    blocks = {(0, -1): 0, (-1, -1): 1, (1, -1): 2, (0, 1): 3, (-1, 1): 4, (1, 1): 5}

    def exchange(index, shifts):
        made = []
        for i, side in enumerate(SIDES):
            dk, dr = side
            if dr == 0:
                src = shifts.at[1, :, slot(1 if dk < 0 else tile_cols)]
                dst = shifts.at[1, :, slot(tile_cols + 1 if dk < 0 else 0)]
            else:
                src = edge_out.at[index, pl.ds(0 if dr < 0 else PACK, PACK), :]
                dst = edge_in.at[index, pl.ds(PACK * blocks[(-dk, -dr)], PACK), :]
            made.append(
                pltpu.make_async_remote_copy(
                    src_ref=src,
                    dst_ref=dst,
                    send_sem=x_send.at[index, i],
                    recv_sem=x_recv.at[index, i],
                    device_id=(gid, k + dk, r + dr),
                    device_id_type=MESH,
                )
            )
        return made

    def opposite(i):
        return SIDES.index((-SIDES[i][0], -SIDES[i][1]))

    def send_edges(index, shifts):
        made = exchange(index, shifts)
        for i in (3, 2, 0, 1, 4, 5, 6, 7):
            @pl.when(there(SIDES[i]))
            def _():
                made[i].start()

    def await_edges(index, shifts):
        made = exchange(index, shifts)
        for i, side in enumerate(SIDES):
            @pl.when(there(side))
            def _():
                made[opposite(i)].wait_recv()

    def await_sent(index, shifts):
        made = exchange(index, shifts)
        for i, side in enumerate(SIDES):
            @pl.when(there(side))
            def _():
                made[i].wait_send()

    def clear_edges(index, shifts):
        for side in SIDES:
            dk, dr = side

            @pl.when(jnp.logical_not(there(side)))
            def _():
                if dr == 0:
                    shifts[1, :, slot(0 if dk < 0 else tile_cols + 1)] = jnp.zeros((C, LANE), BF)
                else:
                    edge_in[index, pl.ds(PACK * blocks[side], PACK), :] = jnp.zeros(
                        (PACK, edge_in.shape[2]), BF
                    )

    def pack_column(edges, w, value):
        edges = jnp.where(lane == w + 1, value[:, 0:1], edges)
        return jnp.where(lane == PACK + w + 1, value[:, LANE - 1 : LANE], edges)

    def store_edges(index, edges):
        spare = edge_out.shape[2] - C
        tall = jnp.concatenate([edges, jnp.zeros((spare, LANE), F32)], axis=0)
        edge_out[index] = tall.T[: 2 * PACK].astype(BF)

    def make_shifts(index, shifts):
        halo = edge_in[index].astype(F32).T[:C]
        for s in range(tile_cols + 2):
            if s == 0:
                at = PACK + tile_cols
            elif s == tile_cols + 1:
                at = 2 * PACK + 1
            else:
                at = s
            value = shifts[1, :, slot(s)].astype(F32)
            before = jnp.where(lane == 0, halo[:, at : at + 1], pltpu.roll(value, 1, 1))
            at += 3 * PACK
            after = jnp.where(
                lane == LANE - 1, halo[:, at : at + 1], pltpu.roll(value, LANE - 1, 1)
            )
            shifts[0, :, slot(s)] = before.astype(BF)
            shifts[2, :, slot(s)] = after.astype(BF)

    def pack_weights(i):
        loads[2 + i].wait()
        for t in range(9):
            packed[i, :, pl.ds(t * main, main)] = raw[i, t, :, :main]
        for t in range(0, 9, 2):
            here = raw[i, t, :, main:]
            at = 9 * main + t * rest
            if t < 8:
                here = jnp.concatenate([here, raw[i, t + 1, :, main:]], axis=1)
            packed[i, :, pl.ds(at, here.shape[1])] = here

    def convolve(i, shifts, q):
        pieces, last = [], []
        for t in range(9):
            at = pl.ds(pl.multiple_of((q * strip_cols + t // 3) * LANE, LANE), wide)
            pieces.append(shifts[t % 3, :main, at])
            last.append(shifts[t % 3, main:, at])
        patch = jnp.concatenate(pieces + last, axis=0)
        total = jnp.dot(packed[i], patch, preferred_element_type=F32)
        return total + jnp.concatenate([biases[i]] * strip_cols, axis=1)

    def part(q):
        return pl.ds(pl.multiple_of(q * wide, LANE), wide)

    def inner(q):
        return pl.ds(pl.multiple_of(q * wide + LANE, LANE), wide)

    loads[0].wait()
    edges = jnp.zeros((C, LANE), F32)
    for w in range(tile_cols):
        value = base[:, w, :].astype(BF)
        shifts_b[1, :, slot(w + 1)] = value
        edges = pack_column(edges, w, value.astype(F32))
    store_edges(0, edges)
    entered()
    send_edges(0, shifts_b)

    loads[1].wait()
    for q in range(n_rows):
        strips[q] = jnp.concatenate(
            [control[:, w, pl.ds(q * LANE, LANE)] for w in range(strip_cols)], axis=1
        ).astype(BF)

    def to_tile(j, o):
        q, _ = partner(o)
        return pltpu.make_async_remote_copy(
            src_ref=strips.at[q],
            dst_ref=shifts_c.at[1, :, inner(r)],
            send_sem=in_send.at[j],
            recv_sem=in_recv.at[j],
            device_id=(gid, k, q),
            device_id_type=MESH,
        )

    def to_strip(j, o):
        q, _ = partner(o)
        return pltpu.make_async_remote_copy(
            src_ref=bracket.at[q],
            dst_ref=arrived.at[r],
            send_sem=out_send.at[j],
            recv_sem=out_recv.at[j],
            device_id=(gid, k, q),
            device_id_type=MESH,
        )

    for j, o in enumerate(order):
        to_tile(j, o).start()
    shifts_c[1, :, inner(r)] = strips[r]

    for i, (index, ref) in enumerate(((0, b1_ref), (1, b2_ref), (2, bc_ref))):
        row = jnp.concatenate([ref[...][None], jnp.zeros((1, edge_out.shape[2] - C), F32)], axis=1)
        biases[i] = jnp.broadcast_to(row, (LANE, edge_out.shape[2])).T[:C]
    for index, shifts in enumerate((shifts_b, shifts_h, shifts_c)):
        clear_edges(index, shifts)
    pack_weights(0)

    await_edges(0, shifts_b)
    make_shifts(0, shifts_b)
    edges = jnp.zeros((C, LANE), F32)
    for q in range(n_rows):
        value = silu(convolve(0, shifts_b, q)).astype(BF)
        shifts_h[1, :, pl.ds(q * wide + LANE, wide)] = value
        for w in range(strip_cols):
            edges = pack_column(
                edges, q * strip_cols + w, value[:, w * LANE : (w + 1) * LANE].astype(F32)
            )
    store_edges(1, edges)
    send_edges(1, shifts_h)
    pack_weights(1)
    pack_weights(2)

    for j, o in enumerate(order):
        to_tile(j, o).wait_recv()
    edges = jnp.zeros((C, LANE), F32)
    for w in range(tile_cols):
        edges = pack_column(edges, w, shifts_c[1, :, slot(w + 1)].astype(F32))
    store_edges(2, edges)
    send_edges(2, shifts_c)

    await_edges(1, shifts_h)
    make_shifts(1, shifts_h)
    for q in range(n_rows):
        own = jnp.concatenate([base[:, q * strip_cols + w, :] for w in range(strip_cols)], axis=1)
        mid[:, pl.ds(q * wide, wide)] = silu(convolve(1, shifts_h, q)) + own

    await_edges(2, shifts_c)
    make_shifts(2, shifts_c)
    for j, o in enumerate(order + [0]):
        q = partner(o)[0] if o else r
        here = mid[:, part(q)]
        change = silu(convolve(2, shifts_c, q)) + jnp.dot(
            tc_ref[...], here.astype(BF), preferred_element_type=F32
        )
        bracket[q] = change.astype(BF)
        if o:
            to_strip(j, o).start()
        send = (change + shifts_c[1, :, inner(q)].astype(F32)).astype(BF)
        result[:, part(q)] = here + jnp.dot(tb_ref[...], send, preferred_element_type=F32)
    arrived[r] = bracket[r]

    for w in range(tile_cols):
        base_out[pl.ds(w, C, tile_cols), :] = result[:, slot(w)]
    for j, o in enumerate(order):
        to_strip(j, o).wait_recv()
    for q in range(n_rows):
        for w in range(strip_cols):
            at = pl.ds(q * LANE, LANE)
            control_out[:, w, at] = control[:, w, at] + arrived[q, :, slot(w)].astype(F32)
    for index, shifts in enumerate((shifts_b, shifts_h, shifts_c)):
        await_sent(index, shifts)
    for j, o in enumerate(order):
        to_tile(j, o).wait_send()
        to_strip(j, o).wait_send()


def solution(mesh):
    n_cols, n_rows = mesh.shape["cols"], mesh.shape["rows"]

    def per_device(base, control, k1, k2, kc, b1, b2, bc, tc, tb):
        C, tile_cols, _ = base.shape
        strip_cols = control.shape[1]
        wide = strip_cols * LANE
        tall = -(-C // LANE) * LANE
        area = tile_cols * LANE
        held = pltpu.VMEM((3, C, area + 2 * LANE), BF)
        others = n_rows - 1
        any_spec = pl.BlockSpec(memory_space=pl.ANY)
        vmem = pl.BlockSpec(memory_space=pltpu.VMEM)
        base_new, control_new = pl.pallas_call(
            functools.partial(kernel, n_cols, n_rows),
            out_shape=(
                jax.ShapeDtypeStruct((C * tile_cols, LANE), F32),
                jax.ShapeDtypeStruct(control.shape, F32),
            ),
            in_specs=[any_spec] * 5 + [vmem] * 5,
            out_specs=(vmem, vmem),
            scratch_shapes=[
                pltpu.VMEM(base.shape, F32),
                pltpu.VMEM(control.shape, F32),
                pltpu.VMEM((3,) + k1.shape, BF),
                pltpu.VMEM((3, C, 9 * C), BF),
                held,
                held,
                held,
                pltpu.VMEM((3, C, LANE), F32),
                pltpu.VMEM((3, 2 * PACK, tall), BF),
                pltpu.VMEM((3, LANE, tall), BF),
                pltpu.VMEM((n_rows, C, wide), BF),
                pltpu.VMEM((C, area), F32),
                pltpu.VMEM((C, area), F32),
                pltpu.VMEM((n_rows, C, wide), BF),
                pltpu.VMEM((n_rows, C, wide), BF),
                pltpu.SemaphoreType.DMA((5,)),
                pltpu.SemaphoreType.DMA((3, 8)),
                pltpu.SemaphoreType.DMA((3, 8)),
                pltpu.SemaphoreType.DMA((others,)),
                pltpu.SemaphoreType.DMA((others,)),
                pltpu.SemaphoreType.DMA((others,)),
                pltpu.SemaphoreType.DMA((others,)),
            ],
            compiler_params=pltpu.CompilerParams(
                collective_id=0, has_side_effects=True, vmem_limit_bytes=60 * 1024 * 1024
            ),
        )(base, control, k1, k2, kc, b1, b2, bc, tc, tb)
        return base_new.reshape(base.shape), control_new

    tiles = P(None, ("groups", "cols"), "rows")
    lines = P(None, ("groups", "cols", "rows"), None)
    return jax.shard_map(
        per_device,
        mesh=mesh,
        in_specs=(tiles, lines) + (P(),) * 8,
        out_specs=(tiles, lines),
        check_vma=False,
    )
```

profile of v0, /device:TPU:0, one launch (start us, length us, event | category | flops | bytes accessed | tf_op | source)
XLA Modules:
  0.0 42.5 jit_solution(12084068678179181644)
XLA Ops:
  0.6 38.2 %shard_map.113 = (f32[2560,128]{1,0:T(8,128)}, f32[320,2,512]{2,1,0:T(2,128)}) custom-call(f32[320,8,128]{2,1,0:T(8,128)} %base_hbm.1, f32[320,2,512]{2,1,0:T(2,128)} %control_hbm.1, bf16[9,320,320]{2,1,0:T(8,128)(2,1)} %k1_hbm.1, bf16[9,320,320]{2,1,0:T(8,128)(2,1)} %k2_hbm.1, bf16[9,320,320]{2,1,0:T(8,128)(2,1)} %kc_hbm.1, f32[320]{0:T(512)} %b1_ref.1, ...), custom_call_target="tpu_custom_call" | custom-call | tf_op jit(solution)/shard_map/pallas_call | solution.py:363
  38.8 0.0 copy-start
  38.8 2.6 %copy.14 = f32[320,8,128]{2,1,0:T(8,128)} copy(f32[320,8,128]{2,1,0:T(8,128)} %bitcast.1) | data formatting | bytes 2621440
  41.4 0.0 copy-done
  41.4 1.1 %copy.15 = f32[320,2,512]{2,1,0:T(2,128)} copy(f32[320,2,512]{2,1,0:T(2,128)S(1)} %copy-done) | data formatting | bytes 2621440
Async XLA Ops:
  38.8 2.6 %copy-start = (f32[320,2,512]{2,1,0:T(2,128)S(1)}, f32[320,2,512]{2,1,0:T(2,128)}, u32[]{:S(2)}) copy-start(f32[320,2,512]{2,1,0:T(2,128)} %get-tuple-element.9) | copy-start | bytes 3932164
where the time goes:
time: 43 us; the launch traced here: 42.5 us
  Pallas kernels  38.2 us (89%)
  local copies, waits for them, and re-layouts  3.62 us (8%)
  between operations  0.65 us (2%)
    pallas_call x1, Pallas kernels, per_device(): pl.pallas_call(functools.partial(kernel, n_cols, n_rows), out_shape=(jax....  38.2 us
    unnamed x4, local copies, waits for them, and re-layouts  3.62 us

commit v1 on v0

v1 whole, which is shorter than its diff:
```python
import functools

import jax
import jax.numpy as jnp
from jax import lax
from jax.experimental import pallas as pl
from jax.experimental.pallas import tpu as pltpu
from jax.sharding import PartitionSpec as P

MESH = pl.DeviceIdType.MESH
BF = jnp.bfloat16
F32 = jnp.float32
LANE = 128
PACK = 16
SIDES = ((-1, 0), (1, 0), (0, -1), (0, 1), (-1, -1), (1, -1), (-1, 1), (1, 1))
NT = (((1,), (1,)), ((), ()))


def silu(v):
    return 0.5 * v * (1.0 + jnp.tanh(0.5 * v))


def kernel(
    n_cols,
    n_rows,
    base_hbm,
    control_hbm,
    k1_hbm,
    k2_hbm,
    kc_hbm,
    b1_hbm,
    b2_hbm,
    bc_hbm,
    tc_hbm,
    tb_hbm,
    base_new,
    ctl,
    base,
    raw,
    packed,
    shifts_b,
    shifts_h,
    shifts_c,
    row1,
    row2,
    row3,
    biases,
    tc_ref,
    tb_ref,
    edge_out,
    edge_in,
    cedge_out,
    cedge_in,
    strips,
    mid,
    inner_mid,
    bracket,
    arrived,
    load_sem,
    x_send,
    x_recv,
    in_send,
    in_recv,
    ce_send,
    ce_recv,
    fw_send,
    fw_recv,
    out_send,
    out_recv,
):
    C = tc_ref.shape[0]
    tile_cols = base.shape[0] // C
    strip_cols = ctl.shape[2]
    wide = strip_cols * LANE
    main = C - C % LANE
    rest = C - main
    tall = edge_out.shape[2]
    half = n_rows // 2
    half_cols = half * strip_cols
    gid = lax.axis_index("groups")
    k = lax.axis_index("cols")
    r = lax.axis_index("rows")
    lane = lax.broadcasted_iota(jnp.int32, (C, LANE), 1)
    flat = ctl.reshape(n_rows * C * strip_cols, LANE)

    near_base = half * lax.div(r, half)
    far_base = half - near_base
    far_is_left = lax.div(r, half)
    near_start = near_base * strip_cols
    far_start = far_base * strip_cols
    buddies = [near_base + lax.rem(r - near_base + o, half) for o in range(1, half)]
    fars = [far_base + j for j in range(half)]

    def load(i, src, dst):
        copy = pltpu.make_async_copy(src, dst, load_sem.at[i])
        copy.start()
        return copy

    base_load = load(0, base_hbm, base)
    ctl_loads = [
        load(1 + q, control_hbm.at[:, :, pl.ds(q * LANE, LANE)], ctl.at[q]) for q in range(n_rows)
    ]
    more = 1 + n_rows
    weight_loads = [load(more, k1_hbm, raw.at[0])]
    row_loads = [
        load(more + 3 + i, src, dst)
        for i, (src, dst) in enumerate(((b1_hbm, row1), (b2_hbm, row2), (bc_hbm, row3)))
    ]
    weight_loads.append(load(more + 2, kc_hbm, raw.at[2]))
    weight_loads.insert(1, load(more + 1, k2_hbm, raw.at[1]))
    t_loads = [load(more + 6, tc_hbm, tc_ref), load(more + 7, tb_hbm, tb_ref)]

    def there(side):
        dk, dr = side
        ok = None
        for at, step, count in ((k, dk, n_cols), (r, dr, n_rows)):
            if step:
                test = (at > 0) if step < 0 else (at < count - 1)
                ok = test if ok is None else jnp.logical_and(ok, test)
        return ok

    barrier = pltpu.get_barrier_semaphore()
    peers = n_rows - 1
    for side in SIDES:
        if side[0]:
            peers = peers + jnp.where(there(side), 1, 0)

            @pl.when(there(side))
            def _():
                pl.semaphore_signal(
                    barrier, inc=1, device_id=(gid, k + side[0], r + side[1]), device_id_type=MESH
                )
    for o in range(1, n_rows):
        pl.semaphore_signal(
            barrier, inc=1, device_id=(gid, k, lax.rem(r + o, n_rows)), device_id_type=MESH
        )

    def slot(s, count=1):
        at = s * LANE
        if not isinstance(at, int):
            at = pl.multiple_of(at, LANE)
        return pl.ds(at, count * LANE)

    blocks = {(0, -1): 0, (-1, -1): 1, (1, -1): 2, (0, 1): 3, (-1, 1): 4, (1, 1): 5}

    def exchange(index, shifts):
        made = []
        for i, side in enumerate(SIDES):
            dk, dr = side
            if dr == 0:
                src = shifts.at[1, :, slot(1 if dk < 0 else tile_cols)]
                dst = shifts.at[1, :, slot(tile_cols + 1 if dk < 0 else 0)]
            else:
                src = edge_out.at[index, pl.ds(0 if dr < 0 else PACK, PACK), :]
                dst = edge_in.at[index, pl.ds(PACK * blocks[(-dk, -dr)], PACK), :]
            made.append(
                pltpu.make_async_remote_copy(
                    src_ref=src,
                    dst_ref=dst,
                    send_sem=x_send.at[index, i],
                    recv_sem=x_recv.at[index, i],
                    device_id=(gid, k + dk, r + dr),
                    device_id_type=MESH,
                )
            )
        return made

    def opposite(i):
        return SIDES.index((-SIDES[i][0], -SIDES[i][1]))

    def send_edges(index, shifts):
        made = exchange(index, shifts)
        for i in (3, 2, 0, 1, 4, 5, 6, 7):
            @pl.when(there(SIDES[i]))
            def _():
                made[i].start()

    def await_edges(index, shifts):
        made = exchange(index, shifts)
        for i, side in enumerate(SIDES):
            @pl.when(there(side))
            def _():
                made[opposite(i)].wait_recv()

    def await_sent(index, shifts):
        made = exchange(index, shifts)
        for i, side in enumerate(SIDES):
            @pl.when(there(side))
            def _():
                made[i].wait_send()

    def clear_edges(index, shifts):
        for side in SIDES:
            dk, dr = side

            @pl.when(jnp.logical_not(there(side)))
            def _():
                if dr == 0:
                    shifts[1, :, slot(0 if dk < 0 else tile_cols + 1)] = jnp.zeros((C, LANE), BF)
                else:
                    edge_in[index, pl.ds(PACK * blocks[side], PACK), :] = jnp.zeros((PACK, tall), BF)

    def edge_picker(first, count):
        row = lax.broadcasted_iota(jnp.int32, (2 * PACK, count * LANE), 0)
        at = lax.broadcasted_iota(jnp.int32, (2 * PACK, count * LANE), 1)
        low = jnp.where(row < PACK, (row - 1 - first) * LANE, (row - PACK - first) * LANE - 1)
        real = jnp.where(row < PACK, row, row - PACK)
        hit = jnp.logical_and(at == low, jnp.logical_and(real > first, real <= first + count))
        return jnp.where(hit, 1.0, 0.0).astype(BF)

    def pad_rows(value):
        return jnp.concatenate([value, jnp.zeros((value.shape[0], tall - C), F32)], axis=1).astype(BF)

    def shift(shifts, s, halo, low, high):
        value = shifts[1, :, slot(s)].astype(F32)
        before = jnp.where(lane == 0, low(halo), pltpu.roll(value, 1, 1))
        after = jnp.where(lane == LANE - 1, high(halo), pltpu.roll(value, LANE - 1, 1))
        shifts[0, :, slot(s)] = before.astype(BF)
        shifts[2, :, slot(s)] = after.astype(BF)

    def shift_fixed(index, shifts, s, halo):
        if s == 0:
            at = PACK + tile_cols
        elif s == tile_cols + 1:
            at = 2 * PACK + 1
        else:
            at = s
        shift(
            shifts,
            s,
            halo,
            lambda h: h[:, at : at + 1],
            lambda h: h[:, at + 3 * PACK : at + 3 * PACK + 1],
        )

    def halo_of(ref):
        return ref[...].astype(F32).T[:C]

    def control_halo(start, count, outer):
        parts = []
        if count:
            parts.append(cedge_in[pl.ds(pl.multiple_of(PACK * start, PACK), PACK * count), :])
        if outer is not None:
            parts.append(cedge_in[pl.ds(pl.multiple_of(PACK * outer, PACK), PACK), :])
        parts = [part.astype(F32) for part in parts]
        have = sum(part.shape[0] for part in parts)
        parts.append(jnp.zeros((LANE - have, tall), F32))
        return jnp.concatenate(parts, axis=0).T[:C]

    def shift_control(s, at, halo):
        shift(shifts_c, s, halo, lambda h: h[:, at : at + 1], lambda h: h[:, at + 1 : at + 2])

    def shift_half(start, halo):
        for c in range(half_cols):
            at = PACK * (c // strip_cols) + 2 * (c % strip_cols)
            shift_control(start + c + 1, at, halo)

    def shift_outer(on_left, at, halo):
        value = jnp.where(on_left == 1, pltpu.roll(halo, LANE - 2 * (strip_cols - 1), 1), halo)
        shift_control((1 - on_left) * (tile_cols + 1), at, value)

    def pack_weights(i):
        weight_loads[i].wait()
        for t in range(9):
            packed[i, :, pl.ds(t * main, main)] = raw[i, t, :, :main]
        for t in range(0, 9, 2):
            here = raw[i, t, :, main:]
            at = 9 * main + t * rest
            if t < 8:
                here = jnp.concatenate([here, raw[i, t + 1, :, main:]], axis=1)
            packed[i, :, pl.ds(at, here.shape[1])] = here

    def convolve(i, shifts, runs):
        pieces, last = [], []
        for t in range(9):
            top = [shifts[t % 3, :main, slot(c + t // 3, n)] for c, n in runs]
            low = [shifts[t % 3, main:, slot(c + t // 3, n)] for c, n in runs]
            pieces.append(jnp.concatenate(top, axis=1) if len(top) > 1 else top[0])
            last.append(jnp.concatenate(low, axis=1) if len(low) > 1 else low[0])
        patch = jnp.concatenate(pieces + last, axis=0)
        total = jnp.dot(packed[i], patch, preferred_element_type=F32)
        count = sum(n for _, n in runs)
        return silu(total + jnp.concatenate([biases[i]] * count, axis=1))

    base_load.wait()
    for w in range(tile_cols):
        shifts_b[1, :, slot(w + 1)] = base[pl.ds(w, C, tile_cols), :].astype(BF)
    edge_out[0] = pad_rows(
        lax.dot_general(
            edge_picker(0, tile_cols),
            shifts_b[1, :, slot(1, tile_cols)],
            NT,
            preferred_element_type=F32,
        )
    )
    pl.semaphore_wait(barrier, peers)
    send_edges(0, shifts_b)

    def make_strip(q):
        for w in range(strip_cols):
            strips[q, :, w * LANE : (w + 1) * LANE] = flat[
                pl.ds(q * C * strip_cols + w, C, strip_cols), :
            ].astype(BF)

    def to_tile(q, w):
        return pltpu.make_async_remote_copy(
            src_ref=strips.at[q, :, slot(w)],
            dst_ref=shifts_c.at[1, :, slot(r * strip_cols + w + 1)],
            send_sem=in_send.at[q, w],
            recv_sem=in_recv.at[r, w],
            device_id=(gid, k, q),
            device_id_type=MESH,
        )

    def from_strip(q, w):
        return pltpu.make_async_remote_copy(
            src_ref=strips.at[q, :, slot(w)],
            dst_ref=shifts_c.at[1, :, slot(q * strip_cols + w + 1)],
            send_sem=in_send.at[q, w],
            recv_sem=in_recv.at[q, w],
            device_id=(gid, k, q),
            device_id_type=MESH,
        )

    def control_edges(q, to):
        return pltpu.make_async_remote_copy(
            src_ref=cedge_out.at[q],
            dst_ref=cedge_in.at[pl.ds(pl.multiple_of(PACK * (1 + to), PACK), PACK), :],
            send_sem=ce_send.at[q],
            recv_sem=ce_recv.at[to],
            device_id=(gid, k, q),
            device_id_type=MESH,
        )

    def forward(i):
        to_left = far_is_left if i else 1 - far_is_left
        step = 1 - 2 * to_left
        src_slot = 1 + (1 - to_left) * (tile_cols - 1)
        dst_slot = to_left * (tile_cols + 1)
        src_block = 1 + (1 - to_left) * (n_rows - 1)
        dst_block = to_left * (n_rows + 1)
        made = (
            pltpu.make_async_remote_copy(
                src_ref=shifts_c.at[1, :, slot(src_slot)],
                dst_ref=shifts_c.at[1, :, slot(dst_slot)],
                send_sem=fw_send.at[i, 0],
                recv_sem=fw_recv.at[i, 0],
                device_id=(gid, k + step, r),
                device_id_type=MESH,
            ),
            pltpu.make_async_remote_copy(
                src_ref=cedge_in.at[pl.ds(pl.multiple_of(PACK * src_block, PACK), PACK), :],
                dst_ref=cedge_in.at[pl.ds(pl.multiple_of(PACK * dst_block, PACK), PACK), :],
                send_sem=fw_send.at[i, 1],
                recv_sem=fw_recv.at[i, 1],
                device_id=(gid, k + step, r),
                device_id_type=MESH,
            ),
        )
        goes = jnp.where(to_left == 1, k > 0, k < n_cols - 1)
        comes = jnp.where(to_left == 1, k < n_cols - 1, k > 0)
        return made, goes, comes

    def forward_start(i):
        made, goes, _ = forward(i)

        @pl.when(goes)
        def _():
            for copy in made:
                copy.start()

    def forward_recv(i):
        made, _, comes = forward(i)

        @pl.when(comes)
        def _():
            for copy in made:
                copy.wait_recv()

    def forward_sent(i):
        made, goes, _ = forward(i)

        @pl.when(goes)
        def _():
            for copy in made:
                copy.wait_send()

    def to_strip(q, source):
        return pltpu.make_async_remote_copy(
            src_ref=bracket.at[q],
            dst_ref=arrived.at[source],
            send_sem=out_send.at[q],
            recv_sem=out_recv.at[source],
            device_id=(gid, k, q),
            device_id_type=MESH,
        )

    for copy in ctl_loads:
        copy.wait()
    for q in fars:
        make_strip(q)
    for w in range(strip_cols):
        to_tile(fars[0], w).start()
    for q in buddies:
        make_strip(q)
        for w in range(strip_cols):
            to_tile(q, w).start()
    make_strip(r)
    shifts_c[1, :, slot(r * strip_cols + 1, strip_cols)] = strips[r]

    row = lax.broadcasted_iota(jnp.int32, (2 * PACK, wide), 0)
    at = lax.broadcasted_iota(jnp.int32, (2 * PACK, wide), 1)
    real = jnp.where(row < PACK, row, row - PACK)
    w_of = lax.div(real, 2)
    want = jnp.where(row < PACK, w_of * LANE + LANE - 1, w_of * LANE)
    parity = jnp.where(row < PACK, 0, 1)
    hit = jnp.logical_and(at == want, jnp.logical_and(lax.rem(real, 2) == parity, w_of < strip_cols))
    picker = jnp.where(hit, 1.0, 0.0).astype(BF)
    found = [
        lax.dot_general(picker, strips[q], NT, preferred_element_type=F32) for q in range(n_rows)
    ]
    for q in range(n_rows):
        value = None
        if q > 0:
            value = found[q - 1][:PACK]
        if q < n_rows - 1:
            value = found[q + 1][PACK:] if value is None else value + found[q + 1][PACK:]
        cedge_out[q] = pad_rows(value)
    for q in buddies + fars:
        control_edges(q, r).start()
    cedge_in[pl.ds(pl.multiple_of(PACK * (1 + r), PACK), PACK), :] = cedge_out[r]
    for q in fars[1:-1]:
        for w in range(strip_cols):
            to_tile(q, w).start()
    if half > 1:
        to_tile(fars[-1], 0).start()

    for copy in row_loads:
        copy.wait()
    for i, ref in enumerate((row1, row2, row3)):
        line = jnp.concatenate([ref[...][None], jnp.zeros((1, tall - C), F32)], axis=1)
        biases[i] = jnp.broadcast_to(line, (LANE, tall)).T[:C]
    for index, shifts in enumerate((shifts_b, shifts_h)):
        clear_edges(index, shifts)

    @pl.when(k == 0)
    def _():
        shifts_c[1, :, slot(0)] = jnp.zeros((C, LANE), BF)
        cedge_in[pl.ds(0, PACK), :] = jnp.zeros((PACK, tall), BF)

    @pl.when(k == n_cols - 1)
    def _():
        shifts_c[1, :, slot(tile_cols + 1)] = jnp.zeros((C, LANE), BF)
        cedge_in[pl.ds(PACK * (n_rows + 1), PACK), :] = jnp.zeros((PACK, tall), BF)

    pack_weights(0)

    await_edges(0, shifts_b)
    halo = halo_of(edge_in.at[0])
    ready = 0
    edges = None
    for q in range(n_rows):
        while ready < (q + 1) * strip_cols + 2:
            shift_fixed(0, shifts_b, ready, halo)
            ready += 1
        value = convolve(0, shifts_b, [(q * strip_cols, strip_cols)]).astype(BF)
        shifts_h[1, :, slot(q * strip_cols + 1, strip_cols)] = value
        part = lax.dot_general(
            edge_picker(q * strip_cols, strip_cols), value, NT, preferred_element_type=F32
        )
        edges = part if edges is None else edges + part
    edge_out[1] = pad_rows(edges)
    send_edges(1, shifts_h)
    for w in range(1 if half > 1 else 0, strip_cols):
        if half > 1:
            to_tile(fars[-1], w).start()

    pack_weights(2)
    for q in buddies:
        for w in range(strip_cols):
            from_strip(q, w).wait_recv()
        control_edges(q, q).wait_recv()
    forward_start(0)
    shift_half(near_start, control_halo(1 + near_base, half, None))
    inner = []
    left = half_cols - 2
    while left > 0:
        take = min(left, strip_cols)
        inner.append([(near_start + half_cols - 1 - left, take)])
        left -= take
    for i, runs in enumerate(inner):
        inner_mid[i, :, : runs[0][1] * LANE] = convolve(2, shifts_c, runs)
    pack_weights(1)

    await_edges(1, shifts_h)
    halo = halo_of(edge_in.at[1])
    for s in range(tile_cols + 2):
        shift_fixed(1, shifts_h, s, halo)

    def second(start):
        own = jnp.concatenate(
            [base[pl.ds(start + w, C, tile_cols), :] for w in range(strip_cols)], axis=1
        )
        mid[:, slot(start, strip_cols)] = convolve(1, shifts_h, [(start, strip_cols)]) + own

    def columns(ref, runs):
        parts = [ref[:, slot(c, n)] for c, n in runs]
        return jnp.concatenate(parts, axis=1) if len(parts) > 1 else parts[0]

    def change_of(middle, runs):
        return middle + jnp.dot(
            tc_ref[...], columns(mid, runs).astype(BF), preferred_element_type=F32
        )

    def put_base(change, runs):
        control = columns(shifts_c.at[1], [(c + 1, n) for c, n in runs]).astype(F32)
        value = columns(mid, runs) + jnp.dot(
            tb_ref[...], (change + control).astype(BF), preferred_element_type=F32
        )
        done = 0
        for c, n in runs:
            for w in range(n):
                base_new[pl.ds(c + w, C, tile_cols), :] = value[:, done * LANE : (done + 1) * LANE]
                done += 1

    for q in fars:
        second(q * strip_cols)

    for copy in t_loads:
        copy.wait()
    for q in fars:
        for w in range(strip_cols):
            from_strip(q, w).wait_recv()
        control_edges(q, q).wait_recv()
    forward_start(1)
    forward_recv(0)
    halo = control_halo(1 + far_base, half, (1 - far_is_left) * (n_rows + 1))
    shift_half(far_start, halo)
    shift_outer(far_is_left, PACK * half, halo)
    for q in fars:
        runs = [(q * strip_cols, strip_cols)]
        change = change_of(convolve(2, shifts_c, runs), runs)
        bracket[q] = change.astype(BF)
        to_strip(q, r).start()
        put_base(change, runs)

    for i in range(half):
        second((near_base + i) * strip_cols)
    for i, runs in enumerate(inner):
        change = change_of(inner_mid[i, :, : runs[0][1] * LANE], runs)
        for w in range(runs[0][1]):
            col = half_cols - 1 - (half_cols - 2 - i * strip_cols) + w
            bracket[near_base + col // strip_cols, :, slot(col % strip_cols)] = change[
                :, w * LANE : (w + 1) * LANE
            ].astype(BF)
        put_base(change, runs)

    forward_recv(1)
    halo = control_halo(0, 0, far_is_left * (n_rows + 1))
    shift_outer(1 - far_is_left, 0, halo)
    runs = [(near_start, 1), (near_start + half_cols - 1, 1)]
    change = change_of(convolve(2, shifts_c, runs), runs)
    bracket[near_base, :, slot(0)] = change[:, :LANE].astype(BF)
    bracket[near_base + half - 1, :, slot(strip_cols - 1)] = change[:, LANE:].astype(BF)
    for q in buddies:
        to_strip(q, r).start()
    put_base(change, runs)
    arrived[r] = bracket[r]

    def finish(q):
        for w in range(strip_cols):
            where = pl.ds(q * C * strip_cols + w, C, strip_cols)
            flat[where, :] = flat[where, :] + arrived[q, :, slot(w)].astype(F32)

    finish(r)
    for q in buddies + fars:
        to_strip(q, q).wait_recv()
        finish(q)
    for index, shifts in enumerate((shifts_b, shifts_h)):
        await_sent(index, shifts)
    for i in range(2):
        forward_sent(i)
    for q in buddies + fars:
        for w in range(strip_cols):
            to_tile(q, w).wait_send()
        control_edges(q, r).wait_send()
        to_strip(q, r).wait_send()


def deliver(base_new, ctl, base_out, control_out, sem):
    n_rows = ctl.shape[0]
    copies = [pltpu.make_async_copy(base_new, base_out, sem.at[n_rows])]
    for q in range(n_rows):
        copies.append(
            pltpu.make_async_copy(
                ctl.at[q], control_out.at[:, :, pl.ds(q * LANE, LANE)], sem.at[q]
            )
        )
    for copy in copies:
        copy.start()
    for copy in copies:
        copy.wait()


def solution(mesh):
    n_cols, n_rows = mesh.shape["cols"], mesh.shape["rows"]

    def per_device(base, control, k1, k2, kc, b1, b2, bc, tc, tb):
        C, tile_cols, _ = base.shape
        strip_cols = control.shape[1]
        wide = strip_cols * LANE
        tall = -(-C // LANE) * LANE
        area = tile_cols * LANE
        half = n_rows // 2
        held = pltpu.VMEM((3, C, area + 2 * LANE), BF)
        inner = max(1, -(-(half * strip_cols - 2) // strip_cols))
        hbm = pl.BlockSpec(memory_space=pltpu.HBM)
        vmem = pl.BlockSpec(memory_space=pltpu.VMEM)
        base_new, ctl = pl.pallas_call(
            functools.partial(kernel, n_cols, n_rows),
            out_shape=(
                pltpu.VMEM((C * tile_cols, LANE), F32),
                pltpu.VMEM((n_rows, C, strip_cols, LANE), F32),
            ),
            in_specs=[hbm] * 10,
            out_specs=(vmem, vmem),
            scratch_shapes=[
                pltpu.VMEM((C * tile_cols, LANE), F32),
                pltpu.VMEM((3,) + k1.shape, BF),
                pltpu.VMEM((3, C, 9 * C), BF),
                held,
                held,
                held,
                pltpu.VMEM((C,), F32),
                pltpu.VMEM((C,), F32),
                pltpu.VMEM((C,), F32),
                pltpu.VMEM((3, C, LANE), F32),
                pltpu.VMEM((C, C), BF),
                pltpu.VMEM((C, C), BF),
                pltpu.VMEM((2, 2 * PACK, tall), BF),
                pltpu.VMEM((2, LANE, tall), BF),
                pltpu.VMEM((n_rows, PACK, tall), BF),
                pltpu.VMEM((LANE, tall), BF),
                pltpu.VMEM((n_rows, C, wide), BF),
                pltpu.VMEM((C, area), F32),
                pltpu.VMEM((inner, C, wide), F32),
                pltpu.VMEM((n_rows, C, wide), BF),
                pltpu.VMEM((n_rows, C, wide), BF),
                pltpu.SemaphoreType.DMA((9 + n_rows,)),
                pltpu.SemaphoreType.DMA((2, 8)),
                pltpu.SemaphoreType.DMA((2, 8)),
                pltpu.SemaphoreType.DMA((n_rows, strip_cols)),
                pltpu.SemaphoreType.DMA((n_rows, strip_cols)),
                pltpu.SemaphoreType.DMA((n_rows,)),
                pltpu.SemaphoreType.DMA((n_rows,)),
                pltpu.SemaphoreType.DMA((2, 2)),
                pltpu.SemaphoreType.DMA((2, 2)),
                pltpu.SemaphoreType.DMA((n_rows,)),
                pltpu.SemaphoreType.DMA((n_rows,)),
            ],
            compiler_params=pltpu.CompilerParams(
                collective_id=0, has_side_effects=True, vmem_limit_bytes=60 * 1024 * 1024
            ),
        )(base.reshape(C * tile_cols, LANE), control, k1, k2, kc, b1, b2, bc, tc, tb)
        base_out, control_out = pl.pallas_call(
            deliver,
            out_shape=(
                jax.ShapeDtypeStruct(base_new.shape, F32),
                jax.ShapeDtypeStruct(control.shape, F32),
            ),
            in_specs=[vmem] * 2,
            out_specs=(hbm, hbm),
            scratch_shapes=[pltpu.SemaphoreType.DMA((n_rows + 1,))],
            compiler_params=pltpu.CompilerParams(vmem_limit_bytes=1024 * 1024),
        )(base_new, ctl)
        return base_out.reshape(base.shape), control_out

    tiles = P(None, ("groups", "cols"), "rows")
    lines = P(None, ("groups", "cols", "rows"), None)
    return jax.shard_map(
        per_device,
        mesh=mesh,
        in_specs=(tiles, lines) + (P(),) * 8,
        out_specs=(tiles, lines),
        check_vma=False,
    )
```

time: 43 us -> 32.3 us (0.75)
  the two profiles are of different devices: /device:TPU:0 before, /device:TPU:1 now
where the time goes in v1:
time: 32.3 us; the launch traced here: 32.1 us
  Pallas kernels  31.5 us (98%)
  between operations  0.64 us (2%)
    pallas_call x1, Pallas kernels, per_device(): pl.pallas_call(functools.partial(kernel, n_cols, n_rows), out_shape=(pltp...  30 us
    pallas_call x1, Pallas kernels, per_device(): pl.pallas_call(deliver, out_shape=(jax.ShapeDtypeStruct(base_new.shape, F...  1.52 us

profile of v1, /device:TPU:1, one launch (start us, length us, event | category | flops | bytes accessed | tf_op | source)
XLA Modules:
  0.0 32.1 jit_solution(10115952998495006795)
XLA Ops:
  0.6 30.0 %shard_map.113 = (f32[2560,128]{1,0:T(8,128)S(1)}, f32[4,320,2,128]{3,2,1,0:T(2,128)S(1)}) custom-call(f32[2560,128]{1,0:T(8,128)} %bitcast.2, f32[320,2,512]{2,1,0:T(2,128)} %control_hbm.1, bf16[9,320,320]{2,1,0:T(8,128)(2,1)} %k1_hbm.1, bf16[9,320,320]{2,1,0:T(8,128)(2,1)} %k2_hbm.1, bf16[9,320,320]{2,1,0:T(8,128)(2,1)} %kc_hbm.1, f32[320]{0:T(512)} %b1_hbm.1, ...), custom_call_target="tpu_custom_call" | custom-call | tf_op jit(solution)/shard_map/pallas_call | solution.py:619
  30.6 1.5 %shard_map.114 = (f32[2560,128]{1,0:T(8,128)}, f32[320,2,512]{2,1,0:T(2,128)}) custom-call(f32[2560,128]{1,0:T(8,128)S(1)} %get-tuple-element.6.base_new, f32[4,320,2,128]{3,2,1,0:T(2,128)S(1)} %get-tuple-element.7.ctl), custom_call_target="tpu_custom_call" | custom-call | tf_op jit(solution)/shard_map/pallas_call | solution.py:665

commit v2 on v1

--- a/solution.py
+++ b/solution.py
@@ -13,6 +13,8 @@
 LANE = 128
 PACK = 16
 SIDES = ((-1, 0), (1, 0), (0, -1), (0, 1), (-1, -1), (1, -1), (-1, 1), (1, 1))
+ROW_SIDES = ((0, 1), (0, -1))
+WIDE_SIDES = tuple(side for side in SIDES if side[0])
 NT = (((1,), (1,)), ((), ()))
 
 
@@ -54,6 +56,7 @@
     strips,
     mid,
     inner_mid,
+    far_change,
     bracket,
     arrived,
     load_sem,
@@ -77,6 +80,7 @@
     tall = edge_out.shape[2]
     half = n_rows // 2
     half_cols = half * strip_cols
+    assert n_rows == 2 * half and half_cols == strip_cols + 2 and 2 * half_cols == tile_cols
     gid = lax.axis_index("groups")
     k = lax.axis_index("cols")
     r = lax.axis_index("rows")
@@ -90,6 +94,7 @@
     far_start = far_base * strip_cols
     buddies = [near_base + lax.rem(r - near_base + o, half) for o in range(1, half)]
     fars = [far_base + j for j in range(half)]
+    inward = [far_base + j + far_is_left * (half - 1 - 2 * j) for j in range(half)]
 
     def load(i, src, dst):
         copy = pltpu.make_async_copy(src, dst, load_sem.at[i])
@@ -141,11 +146,12 @@
             at = pl.multiple_of(at, LANE)
         return pl.ds(at, count * LANE)
 
-    blocks = {(0, -1): 0, (-1, -1): 1, (1, -1): 2, (0, 1): 3, (-1, 1): 4, (1, 1): 5}
-
-    def exchange(index, shifts):
+    blocks = {(0, -1): 0, (0, 1): 1, (-1, -1): 2, (1, -1): 3, (-1, 1): 4, (1, 1): 5}
+
+    def exchange(index, shifts, which):
         made = []
-        for i, side in enumerate(SIDES):
+        for side in which:
+            i = SIDES.index(side)
             dk, dr = side
             if dr == 0:
                 src = shifts.at[1, :, slot(1 if dk < 0 else tile_cols)]
@@ -165,32 +171,27 @@
             )
         return made
 
-    def opposite(i):
-        return SIDES.index((-SIDES[i][0], -SIDES[i][1]))
-
-    def send_edges(index, shifts):
-        made = exchange(index, shifts)
-        for i in (3, 2, 0, 1, 4, 5, 6, 7):
-            @pl.when(there(SIDES[i]))
-            def _():
-                made[i].start()
-
-    def await_edges(index, shifts):
-        made = exchange(index, shifts)
-        for i, side in enumerate(SIDES):
+    def send_edges(index, shifts, which):
+        for side, copy in zip(which, exchange(index, shifts, which)):
             @pl.when(there(side))
             def _():
-                made[opposite(i)].wait_recv()
-
-    def await_sent(index, shifts):
-        made = exchange(index, shifts)
-        for i, side in enumerate(SIDES):
+                copy.start()
+
+    def await_edges(index, shifts, which):
+        facing = [(-side[0], -side[1]) for side in which]
+        for side, copy in zip(which, exchange(index, shifts, facing)):
             @pl.when(there(side))
             def _():
-                made[i].wait_send()
-
-    def clear_edges(index, shifts):
-        for side in SIDES:
+                copy.wait_recv()
+
+    def await_sent(index, shifts, which):
+        for side, copy in zip(which, exchange(index, shifts, which)):
+            @pl.when(there(side))
+            def _():
+                copy.wait_send()
+
+    def clear_edges(index, shifts, which):
+        for side in which:
             dk, dr = side
 
             @pl.when(jnp.logical_not(there(side)))
@@ -211,30 +212,31 @@
     def pad_rows(value):
         return jnp.concatenate([value, jnp.zeros((value.shape[0], tall - C), F32)], axis=1).astype(BF)
 
+    def move(value, by):
+        by = by % LANE
+        return pltpu.roll(value, by, 1) if by else value
+
     def shift(shifts, s, halo, low, high):
-        value = shifts[1, :, slot(s)].astype(F32)
-        before = jnp.where(lane == 0, low(halo), pltpu.roll(value, 1, 1))
-        after = jnp.where(lane == LANE - 1, high(halo), pltpu.roll(value, LANE - 1, 1))
-        shifts[0, :, slot(s)] = before.astype(BF)
-        shifts[2, :, slot(s)] = after.astype(BF)
-
-    def shift_fixed(index, shifts, s, halo):
-        if s == 0:
-            at = PACK + tile_cols
-        elif s == tile_cols + 1:
-            at = 2 * PACK + 1
-        else:
-            at = s
-        shift(
-            shifts,
-            s,
-            halo,
-            lambda h: h[:, at : at + 1],
-            lambda h: h[:, at + 3 * PACK : at + 3 * PACK + 1],
-        )
-
-    def halo_of(ref):
-        return ref[...].astype(F32).T[:C]
+        value = shifts[1, :, slot(s)]
+        shifts[0, :, slot(s)] = jnp.where(lane == 0, move(halo, -low), move(value, 1))
+        shifts[2, :, slot(s)] = jnp.where(
+            lane == LANE - 1, move(halo, LANE - 1 - high), move(value, -1)
+        )
+
+    def turn(parts):
+        have = sum(part.shape[0] for part in parts)
+        parts = [part.astype(F32) for part in parts] + [jnp.zeros((LANE - have, tall), F32)]
+        return jnp.concatenate(parts, axis=0).T[:C].astype(BF)
+
+    def tile_halo(index, count):
+        return turn([edge_in[index, : PACK * count, :]])
+
+    def shift_inner(shifts, s, halo):
+        shift(shifts, s, halo, s, PACK + s)
+
+    def shift_ends(shifts, halo):
+        shift(shifts, 0, halo, 2 * PACK + tile_cols, 4 * PACK + tile_cols)
+        shift(shifts, tile_cols + 1, halo, 3 * PACK + 1, 5 * PACK + 1)
 
     def control_halo(start, count, outer):
         parts = []
@@ -242,13 +244,10 @@
             parts.append(cedge_in[pl.ds(pl.multiple_of(PACK * start, PACK), PACK * count), :])
         if outer is not None:
             parts.append(cedge_in[pl.ds(pl.multiple_of(PACK * outer, PACK), PACK), :])
-        parts = [part.astype(F32) for part in parts]
-        have = sum(part.shape[0] for part in parts)
-        parts.append(jnp.zeros((LANE - have, tall), F32))
-        return jnp.concatenate(parts, axis=0).T[:C]
+        return turn(parts)
 
     def shift_control(s, at, halo):
-        shift(shifts_c, s, halo, lambda h: h[:, at : at + 1], lambda h: h[:, at + 1 : at + 2])
+        shift(shifts_c, s, halo, at, at + 1)
 
     def shift_half(start, halo):
         for c in range(half_cols):
@@ -256,7 +255,7 @@
             shift_control(start + c + 1, at, halo)
 
     def shift_outer(on_left, at, halo):
-        value = jnp.where(on_left == 1, pltpu.roll(halo, LANE - 2 * (strip_cols - 1), 1), halo)
+        value = jnp.where(on_left == 1, move(halo, -2 * (strip_cols - 1)), halo)
         shift_control((1 - on_left) * (tile_cols + 1), at, value)
 
     def pack_weights(i):
@@ -270,6 +269,16 @@
                 here = jnp.concatenate([here, raw[i, t + 1, :, main:]], axis=1)
             packed[i, :, pl.ds(at, here.shape[1])] = here
 
+    def product(ref, right):
+        middle = C // 2 // PACK * PACK
+        return jnp.concatenate(
+            [
+                jnp.dot(ref[:middle, :], right, preferred_element_type=F32),
+                jnp.dot(ref[middle:, :], right, preferred_element_type=F32),
+            ],
+            axis=0,
+        )
+
     def convolve(i, shifts, runs):
         pieces, last = [], []
         for t in range(9):
@@ -278,7 +287,7 @@
             pieces.append(jnp.concatenate(top, axis=1) if len(top) > 1 else top[0])
             last.append(jnp.concatenate(low, axis=1) if len(low) > 1 else low[0])
         patch = jnp.concatenate(pieces + last, axis=0)
-        total = jnp.dot(packed[i], patch, preferred_element_type=F32)
+        total = product(packed.at[i], patch)
         count = sum(n for _, n in runs)
         return silu(total + jnp.concatenate([biases[i]] * count, axis=1))
 
@@ -294,7 +303,7 @@
         )
     )
     pl.semaphore_wait(barrier, peers)
-    send_edges(0, shifts_b)
+    send_edges(0, shifts_b, ROW_SIDES + WIDE_SIDES)
 
     def make_strip(q):
         for w in range(strip_cols):
@@ -440,8 +449,9 @@
     for i, ref in enumerate((row1, row2, row3)):
         line = jnp.concatenate([ref[...][None], jnp.zeros((1, tall - C), F32)], axis=1)
         biases[i] = jnp.broadcast_to(line, (LANE, tall)).T[:C]
-    for index, shifts in enumerate((shifts_b, shifts_h)):
-        clear_edges(index, shifts)
+    clear_edges(0, shifts_b, ROW_SIDES + WIDE_SIDES)
+    clear_edges(1, shifts_h, ROW_SIDES)
+    clear_edges(2, shifts_h, ROW_SIDES + WIDE_SIDES)
 
     @pl.when(k == 0)
     def _():
@@ -455,25 +465,38 @@
 
     pack_weights(0)
 
-    await_edges(0, shifts_b)
-    halo = halo_of(edge_in.at[0])
-    ready = 0
-    edges = None
-    for q in range(n_rows):
-        while ready < (q + 1) * strip_cols + 2:
-            shift_fixed(0, shifts_b, ready, halo)
+    def hidden(runs):
+        value = convolve(0, shifts_b, runs).astype(BF)
+        total, done = None, 0
+        for c, n in runs:
+            here = value[:, done * LANE : (done + n) * LANE]
+            shifts_h[1, :, slot(c + 1, n)] = here
+            part = lax.dot_general(edge_picker(c, n), here, NT, preferred_element_type=F32)
+            total = part if total is None else total + part
+            done += n
+        return total
+
+    await_edges(0, shifts_b, ROW_SIDES)
+    halo = tile_halo(0, 2)
+    ready, edges, c = 1, None, 1
+    while c < tile_cols - 1:
+        take = min(strip_cols, tile_cols - 1 - c)
+        while ready < c + take + 2:
+            shift_inner(shifts_b, ready, halo)
             ready += 1
-        value = convolve(0, shifts_b, [(q * strip_cols, strip_cols)]).astype(BF)
-        shifts_h[1, :, slot(q * strip_cols + 1, strip_cols)] = value
-        part = lax.dot_general(
-            edge_picker(q * strip_cols, strip_cols), value, NT, preferred_element_type=F32
-        )
+        part = hidden([(c, take)])
         edges = part if edges is None else edges + part
+        c += take
     edge_out[1] = pad_rows(edges)
-    send_edges(1, shifts_h)
-    for w in range(1 if half > 1 else 0, strip_cols):
-        if half > 1:
+    send_edges(1, shifts_h, ROW_SIDES)
+    if half > 1:
+        for w in range(1, strip_cols):
             to_tile(fars[-1], w).start()
+
+    await_edges(0, shifts_b, WIDE_SIDES)
+    shift_ends(shifts_b, tile_halo(0, 6))
+    edge_out[2] = pad_rows(hidden([(0, 1), (tile_cols - 1, 1)]))
+    send_edges(2, shifts_h, ROW_SIDES + WIDE_SIDES)
 
     pack_weights(2)
     for q in buddies:
@@ -492,10 +515,12 @@
         inner_mid[i, :, : runs[0][1] * LANE] = convolve(2, shifts_c, runs)
     pack_weights(1)
 
-    await_edges(1, shifts_h)
-    halo = halo_of(edge_in.at[1])
-    for s in range(tile_cols + 2):
-        shift_fixed(1, shifts_h, s, halo)
+    await_edges(1, shifts_h, ROW_SIDES)
+    halo = tile_halo(1, 2)
+    inner_start = inward[0] * strip_cols
+    rolled = pltpu.roll(halo, lax.rem(LANE - inner_start, LANE), 1)
+    for i in range(strip_cols + 2):
+        shift(shifts_h, inner_start + i, rolled, i, PACK + i)
 
     def second(start):
         own = jnp.concatenate(
@@ -508,23 +533,18 @@
         return jnp.concatenate(parts, axis=1) if len(parts) > 1 else parts[0]
 
     def change_of(middle, runs):
-        return middle + jnp.dot(
-            tc_ref[...], columns(mid, runs).astype(BF), preferred_element_type=F32
-        )
+        return middle + product(tc_ref, columns(mid, runs).astype(BF))
 
     def put_base(change, runs):
         control = columns(shifts_c.at[1], [(c + 1, n) for c, n in runs]).astype(F32)
-        value = columns(mid, runs) + jnp.dot(
-            tb_ref[...], (change + control).astype(BF), preferred_element_type=F32
-        )
+        value = columns(mid, runs) + product(tb_ref, (change + control).astype(BF))
         done = 0
         for c, n in runs:
             for w in range(n):
                 base_new[pl.ds(c + w, C, tile_cols), :] = value[:, done * LANE : (done + 1) * LANE]
                 done += 1
 
-    for q in fars:
-        second(q * strip_cols)
+    second(inner_start)
 
     for copy in t_loads:
         copy.wait()
@@ -533,16 +553,36 @@
             from_strip(q, w).wait_recv()
         control_edges(q, q).wait_recv()
     forward_start(1)
-    forward_recv(0)
-    halo = control_halo(1 + far_base, half, (1 - far_is_left) * (n_rows + 1))
-    shift_half(far_start, halo)
-    shift_outer(far_is_left, PACK * half, halo)
-    for q in fars:
+    shift_half(far_start, control_halo(1 + far_base, half, None))
+
+    def far_part(j):
+        q = inward[j]
         runs = [(q * strip_cols, strip_cols)]
         change = change_of(convolve(2, shifts_c, runs), runs)
         bracket[q] = change.astype(BF)
         to_strip(q, r).start()
-        put_base(change, runs)
+        far_change[j] = change
+
+    far_part(0)
+
+    await_edges(2, shifts_h, ROW_SIDES + WIDE_SIDES)
+    halo_inner = halo
+    halo = tile_halo(2, 6)
+    rest_start = far_is_left * (strip_cols + 2)
+    rolled = pltpu.roll(halo_inner, lax.rem(LANE - 2 - rest_start, LANE), 1)
+    for i in range(tile_cols - 2 - strip_cols - 2):
+        shift(shifts_h, 2 + rest_start + i, rolled, i, PACK + i)
+    shift_inner(shifts_h, 1, halo)
+    shift_inner(shifts_h, tile_cols, halo)
+    shift_ends(shifts_h, halo)
+    for j in range(1, half):
+        second(inward[j] * strip_cols)
+    forward_recv(0)
+    shift_outer(far_is_left, 0, control_halo(0, 0, (1 - far_is_left) * (n_rows + 1)))
+    for j in range(1, half):
+        far_part(j)
+    for j in range(half):
+        put_base(far_change[j], [(inward[j] * strip_cols, strip_cols)])
 
     for i in range(half):
         second((near_base + i) * strip_cols)
@@ -576,8 +616,9 @@
     for q in buddies + fars:
         to_strip(q, q).wait_recv()
         finish(q)
-    for index, shifts in enumerate((shifts_b, shifts_h)):
-        await_sent(index, shifts)
+    await_sent(0, shifts_b, ROW_SIDES + WIDE_SIDES)
+    await_sent(1, shifts_h, ROW_SIDES)
+    await_sent(2, shifts_h, ROW_SIDES + WIDE_SIDES)
     for i in range(2):
         forward_sent(i)
     for q in buddies + fars:
@@ -637,18 +678,19 @@
                 pltpu.VMEM((3, C, LANE), F32),
                 pltpu.VMEM((C, C), BF),
                 pltpu.VMEM((C, C), BF),
-                pltpu.VMEM((2, 2 * PACK, tall), BF),
-                pltpu.VMEM((2, LANE, tall), BF),
+                pltpu.VMEM((3, 2 * PACK, tall), BF),
+                pltpu.VMEM((3, LANE, tall), BF),
                 pltpu.VMEM((n_rows, PACK, tall), BF),
                 pltpu.VMEM((LANE, tall), BF),
                 pltpu.VMEM((n_rows, C, wide), BF),
                 pltpu.VMEM((C, area), F32),
                 pltpu.VMEM((inner, C, wide), F32),
+                pltpu.VMEM((half, C, wide), F32),
                 pltpu.VMEM((n_rows, C, wide), BF),
                 pltpu.VMEM((n_rows, C, wide), BF),
                 pltpu.SemaphoreType.DMA((9 + n_rows,)),
-                pltpu.SemaphoreType.DMA((2, 8)),
-                pltpu.SemaphoreType.DMA((2, 8)),
+                pltpu.SemaphoreType.DMA((3, 8)),
+                pltpu.SemaphoreType.DMA((3, 8)),
                 pltpu.SemaphoreType.DMA((n_rows, strip_cols)),
                 pltpu.SemaphoreType.DMA((n_rows, strip_cols)),
                 pltpu.SemaphoreType.DMA((n_rows,)),

time: 32.3 us -> 27.3 us (0.85)
  the two profiles are of different devices: /device:TPU:1 before, /device:TPU:0 now
where the time goes in v2:
time: 27.3 us; the launch traced here: 27.2 us
  Pallas kernels  26.5 us (97%)
  between operations  0.64 us (2%)
    pallas_call x1, Pallas kernels, per_device(): pl.pallas_call(functools.partial(kernel, n_cols, n_rows), out_shape=(pltp...  25 us
    pallas_call x1, Pallas kernels, per_device(): pl.pallas_call(deliver, out_shape=(jax.ShapeDtypeStruct(base_new.shape, F...  1.52 us

profile of v2, /device:TPU:0, one launch (start us, length us, event | category | flops | bytes accessed | tf_op | source)
XLA Modules:
  0.0 27.2 jit_solution(7930013749036891195)
XLA Ops:
  0.6 25.0 %shard_map.113 = (f32[2560,128]{1,0:T(8,128)S(1)}, f32[4,320,2,128]{3,2,1,0:T(2,128)S(1)}) custom-call(f32[2560,128]{1,0:T(8,128)} %bitcast.2, f32[320,2,512]{2,1,0:T(2,128)} %control_hbm.1, bf16[9,320,320]{2,1,0:T(8,128)(2,1)} %k1_hbm.1, bf16[9,320,320]{2,1,0:T(8,128)(2,1)} %k2_hbm.1, bf16[9,320,320]{2,1,0:T(8,128)(2,1)} %kc_hbm.1, f32[320]{0:T(512)} %b1_hbm.1, ...), custom_call_target="tpu_custom_call" | custom-call | tf_op jit(solution)/shard_map/pallas_call | solution.py:660
  25.7 1.5 %shard_map.114 = (f32[2560,128]{1,0:T(8,128)}, f32[320,2,512]{2,1,0:T(2,128)}) custom-call(f32[2560,128]{1,0:T(8,128)S(1)} %get-tuple-element.6.base_new, f32[4,320,2,128]{3,2,1,0:T(2,128)S(1)} %get-tuple-element.7.ctl), custom_call_target="tpu_custom_call" | custom-call | tf_op jit(solution)/shard_map/pallas_call | solution.py:707

commit v3 on v2

--- a/solution.py
+++ b/solution.py
@@ -15,6 +15,7 @@
 SIDES = ((-1, 0), (1, 0), (0, -1), (0, 1), (-1, -1), (1, -1), (-1, 1), (1, 1))
 ROW_SIDES = ((0, 1), (0, -1))
 WIDE_SIDES = tuple(side for side in SIDES if side[0])
+TAPS = (1, 4, 7, 0, 3, 6, 2, 5, 8)
 NT = (((1,), (1,)), ((), ()))
 
 
@@ -40,9 +41,15 @@
     base,
     raw,
     packed,
-    shifts_b,
-    shifts_h,
-    shifts_c,
+    b_low,
+    b_mid,
+    b_high,
+    h_low,
+    h_mid,
+    h_high,
+    c_low,
+    c_mid,
+    c_high,
     row1,
     row2,
     row3,
@@ -80,6 +87,7 @@
     tall = edge_out.shape[2]
     half = n_rows // 2
     half_cols = half * strip_cols
+    middle = C // 2 // PACK * PACK
     assert n_rows == 2 * half and half_cols == strip_cols + 2 and 2 * half_cols == tile_cols
     gid = lax.axis_index("groups")
     k = lax.axis_index("cols")
@@ -87,6 +95,9 @@
     lane = lax.broadcasted_iota(jnp.int32, (C, LANE), 1)
     flat = ctl.reshape(n_rows * C * strip_cols, LANE)
 
+    shifts_b = (b_low, b_mid, b_high)
+    shifts_h = (h_low, h_mid, h_high)
+    shifts_c = (c_low, c_mid, c_high)
     near_base = half * lax.div(r, half)
     far_base = half - near_base
     far_is_left = lax.div(r, half)
@@ -154,8 +165,8 @@
             i = SIDES.index(side)
             dk, dr = side
             if dr == 0:
-                src = shifts.at[1, :, slot(1 if dk < 0 else tile_cols)]
-                dst = shifts.at[1, :, slot(tile_cols + 1 if dk < 0 else 0)]
+                src = shifts[1].at[:, slot(1 if dk < 0 else tile_cols)]
+                dst = shifts[1].at[:, slot(tile_cols + 1 if dk < 0 else 0)]
             else:
                 src = edge_out.at[index, pl.ds(0 if dr < 0 else PACK, PACK), :]
                 dst = edge_in.at[index, pl.ds(PACK * blocks[(-dk, -dr)], PACK), :]
@@ -197,7 +208,7 @@
             @pl.when(jnp.logical_not(there(side)))
             def _():
                 if dr == 0:
-                    shifts[1, :, slot(0 if dk < 0 else tile_cols + 1)] = jnp.zeros((C, LANE), BF)
+                    shifts[1][:, slot(0 if dk < 0 else tile_cols + 1)] = jnp.zeros((C, LANE), BF)
                 else:
                     edge_in[index, pl.ds(PACK * blocks[side], PACK), :] = jnp.zeros((PACK, tall), BF)
 
@@ -216,10 +227,19 @@
         by = by % LANE
         return pltpu.roll(value, by, 1) if by else value
 
+    def preroll(shifts, s, value):
+        shifts[0][:, slot(s)] = move(value, 1)
+        shifts[2][:, slot(s)] = move(value, -1)
+
+    def mend(shifts, s, halo, low, high):
+        before, after = shifts[0][:, slot(s)], shifts[2][:, slot(s)]
+        shifts[0][:, slot(s)] = jnp.where(lane == 0, move(halo, -low), before)
+        shifts[2][:, slot(s)] = jnp.where(lane == LANE - 1, move(halo, LANE - 1 - high), after)
+
     def shift(shifts, s, halo, low, high):
-        value = shifts[1, :, slot(s)]
-        shifts[0, :, slot(s)] = jnp.where(lane == 0, move(halo, -low), move(value, 1))
-        shifts[2, :, slot(s)] = jnp.where(
+        value = shifts[1][:, slot(s)]
+        shifts[0][:, slot(s)] = jnp.where(lane == 0, move(halo, -low), move(value, 1))
+        shifts[2][:, slot(s)] = jnp.where(
             lane == LANE - 1, move(halo, LANE - 1 - high), move(value, -1)
         )
 
@@ -232,7 +252,7 @@
         return turn([edge_in[index, : PACK * count, :]])
 
     def shift_inner(shifts, s, halo):
-        shift(shifts, s, halo, s, PACK + s)
+        mend(shifts, s, halo, s, PACK + s)
 
     def shift_ends(shifts, halo):
         shift(shifts, 0, halo, 2 * PACK + tile_cols, 4 * PACK + tile_cols)
@@ -259,18 +279,16 @@
         shift_control((1 - on_left) * (tile_cols + 1), at, value)
 
     def pack_weights(i):
-        weight_loads[i].wait()
-        for t in range(9):
-            packed[i, :, pl.ds(t * main, main)] = raw[i, t, :, :main]
-        for t in range(0, 9, 2):
-            here = raw[i, t, :, main:]
-            at = 9 * main + t * rest
-            if t < 8:
-                here = jnp.concatenate([here, raw[i, t + 1, :, main:]], axis=1)
+        for n, t in enumerate(TAPS):
+            packed[i, :, pl.ds(n * main, main)] = raw[i, t, :, :main]
+        for n in range(0, 9, 2):
+            here = raw[i, TAPS[n], :, main:]
+            at = 9 * main + n * rest
+            if n < 8:
+                here = jnp.concatenate([here, raw[i, TAPS[n + 1], :, main:]], axis=1)
             packed[i, :, pl.ds(at, here.shape[1])] = here
 
     def product(ref, right):
-        middle = C // 2 // PACK * PACK
         return jnp.concatenate(
             [
                 jnp.dot(ref[:middle, :], right, preferred_element_type=F32),
@@ -281,9 +299,9 @@
 
     def convolve(i, shifts, runs):
         pieces, last = [], []
-        for t in range(9):
-            top = [shifts[t % 3, :main, slot(c + t // 3, n)] for c, n in runs]
-            low = [shifts[t % 3, main:, slot(c + t // 3, n)] for c, n in runs]
+        for t in TAPS:
+            top = [shifts[t % 3][:main, slot(c + t // 3, n)] for c, n in runs]
+            low = [shifts[t % 3][main:, slot(c + t // 3, n)] for c, n in runs]
             pieces.append(jnp.concatenate(top, axis=1) if len(top) > 1 else top[0])
             last.append(jnp.concatenate(low, axis=1) if len(low) > 1 else low[0])
         patch = jnp.concatenate(pieces + last, axis=0)
@@ -293,11 +311,11 @@
 
     base_load.wait()
     for w in range(tile_cols):
-        shifts_b[1, :, slot(w + 1)] = base[pl.ds(w, C, tile_cols), :].astype(BF)
+        b_mid[:, slot(w + 1)] = base[pl.ds(w, C, tile_cols), :].astype(BF)
     edge_out[0] = pad_rows(
         lax.dot_general(
             edge_picker(0, tile_cols),
-            shifts_b[1, :, slot(1, tile_cols)],
+            b_mid[:, slot(1, tile_cols)],
             NT,
             preferred_element_type=F32,
         )
@@ -311,25 +329,34 @@
                 pl.ds(q * C * strip_cols + w, C, strip_cols), :
             ].astype(BF)
 
-    def to_tile(q, w):
-        return pltpu.make_async_remote_copy(
-            src_ref=strips.at[q, :, slot(w)],
-            dst_ref=shifts_c.at[1, :, slot(r * strip_cols + w + 1)],
-            send_sem=in_send.at[q, w],
-            recv_sem=in_recv.at[r, w],
-            device_id=(gid, k, q),
-            device_id_type=MESH,
-        )
-
-    def from_strip(q, w):
-        return pltpu.make_async_remote_copy(
-            src_ref=strips.at[q, :, slot(w)],
-            dst_ref=shifts_c.at[1, :, slot(q * strip_cols + w + 1)],
-            send_sem=in_send.at[q, w],
-            recv_sem=in_recv.at[q, w],
-            device_id=(gid, k, q),
-            device_id_type=MESH,
-        )
+    def strip_copies(q, to, source):
+        made = []
+        for w in range(strip_cols):
+            for i, (low, count) in enumerate(((0, middle), (middle, C - middle))):
+                made.append(
+                    pltpu.make_async_remote_copy(
+                        src_ref=strips.at[q, pl.ds(low, count), slot(w)],
+                        dst_ref=c_mid.at[
+                            pl.ds(low, count), slot(source * strip_cols + w + 1)
+                        ],
+                        send_sem=in_send.at[q, w, i],
+                        recv_sem=in_recv.at[source, w, i],
+                        device_id=(gid, k, to),
+                        device_id_type=MESH,
+                    )
+                )
+        return made
+
+    def to_tile(q):
+        return strip_copies(q, q, r)
+
+    def from_strip(q):
+        return strip_copies(q, q, q)
+
+    def late_sends(step):
+        if half > 1:
+            for copy in to_tile(fars[-1])[step : 1 if step == 0 else None]:
+                copy.start()
 
     def control_edges(q, to):
         return pltpu.make_async_remote_copy(
@@ -350,8 +377,8 @@
         dst_block = to_left * (n_rows + 1)
         made = (
             pltpu.make_async_remote_copy(
-                src_ref=shifts_c.at[1, :, slot(src_slot)],
-                dst_ref=shifts_c.at[1, :, slot(dst_slot)],
+                src_ref=c_mid.at[:, slot(src_slot)],
+                dst_ref=c_mid.at[:, slot(dst_slot)],
                 send_sem=fw_send.at[i, 0],
                 recv_sem=fw_recv.at[i, 0],
                 device_id=(gid, k + step, r),
@@ -408,14 +435,14 @@
         copy.wait()
     for q in fars:
         make_strip(q)
-    for w in range(strip_cols):
-        to_tile(fars[0], w).start()
+    for copy in to_tile(fars[0]):
+        copy.start()
     for q in buddies:
         make_strip(q)
-        for w in range(strip_cols):
-            to_tile(q, w).start()
+        for copy in to_tile(q):
+            copy.start()
     make_strip(r)
-    shifts_c[1, :, slot(r * strip_cols + 1, strip_cols)] = strips[r]
+    c_mid[:, slot(r * strip_cols + 1, strip_cols)] = strips[r]
 
     row = lax.broadcasted_iota(jnp.int32, (2 * PACK, wide), 0)
     at = lax.broadcasted_iota(jnp.int32, (2 * PACK, wide), 1)
@@ -439,11 +466,8 @@
         control_edges(q, r).start()
     cedge_in[pl.ds(pl.multiple_of(PACK * (1 + r), PACK), PACK), :] = cedge_out[r]
     for q in fars[1:-1]:
-        for w in range(strip_cols):
-            to_tile(q, w).start()
-    if half > 1:
-        to_tile(fars[-1], 0).start()
-
+        for copy in to_tile(q):
+            copy.start()
     for copy in row_loads:
         copy.wait()
     for i, ref in enumerate((row1, row2, row3)):
@@ -455,28 +479,41 @@
 
     @pl.when(k == 0)
     def _():
-        shifts_c[1, :, slot(0)] = jnp.zeros((C, LANE), BF)
+        c_mid[:, slot(0)] = jnp.zeros((C, LANE), BF)
         cedge_in[pl.ds(0, PACK), :] = jnp.zeros((PACK, tall), BF)
 
     @pl.when(k == n_cols - 1)
     def _():
-        shifts_c[1, :, slot(tile_cols + 1)] = jnp.zeros((C, LANE), BF)
+        c_mid[:, slot(tile_cols + 1)] = jnp.zeros((C, LANE), BF)
         cedge_in[pl.ds(PACK * (n_rows + 1), PACK), :] = jnp.zeros((PACK, tall), BF)
 
+    weight_loads[0].wait()
     pack_weights(0)
+    for w in range(tile_cols):
+        preroll(shifts_b, w + 1, b_mid[:, slot(w + 1)])
 
     def hidden(runs):
         value = convolve(0, shifts_b, runs).astype(BF)
         total, done = None, 0
         for c, n in runs:
             here = value[:, done * LANE : (done + n) * LANE]
-            shifts_h[1, :, slot(c + 1, n)] = here
+            h_mid[:, slot(c + 1, n)] = here
+            for w in range(n):
+                preroll(shifts_h, c + 1 + w, here[:, w * LANE : (w + 1) * LANE])
             part = lax.dot_general(edge_picker(c, n), here, NT, preferred_element_type=F32)
             total = part if total is None else total + part
             done += n
         return total
 
+    inner_start = inward[0] * strip_cols
+
     await_edges(0, shifts_b, ROW_SIDES)
+    late_sends(0)
+    for q in buddies:
+        for copy in from_strip(q):
+            copy.wait_recv()
+        control_edges(q, q).wait_recv()
+    forward_start(0)
     halo = tile_halo(0, 2)
     ready, edges, c = 1, None, 1
     while c < tile_cols - 1:
@@ -489,71 +526,49 @@
         c += take
     edge_out[1] = pad_rows(edges)
     send_edges(1, shifts_h, ROW_SIDES)
-    if half > 1:
-        for w in range(1, strip_cols):
-            to_tile(fars[-1], w).start()
+    late_sends(1)
 
     await_edges(0, shifts_b, WIDE_SIDES)
     shift_ends(shifts_b, tile_halo(0, 6))
     edge_out[2] = pad_rows(hidden([(0, 1), (tile_cols - 1, 1)]))
     send_edges(2, shifts_h, ROW_SIDES + WIDE_SIDES)
 
-    pack_weights(2)
-    for q in buddies:
-        for w in range(strip_cols):
-            from_strip(q, w).wait_recv()
-        control_edges(q, q).wait_recv()
-    forward_start(0)
+    for i in (1, 2):
+        weight_loads[i].wait()
+    for i in (1, 2):
+        pack_weights(i)
     shift_half(near_start, control_halo(1 + near_base, half, None))
+    for copy in t_loads:
+        copy.wait()
+
+    def second(start):
+        own = jnp.concatenate(
+            [base[pl.ds(start + w, C, tile_cols), :] for w in range(strip_cols)], axis=1
+        )
+        mid[:, slot(start, strip_cols)] = convolve(1, shifts_h, [(start, strip_cols)]) + own
+
+    def columns(ref, runs):
+        parts = [ref[:, slot(c, n)] for c, n in runs]
+        return jnp.concatenate(parts, axis=1) if len(parts) > 1 else parts[0]
+
+    def change_of(middle, runs):
+        return middle + product(tc_ref, columns(mid, runs).astype(BF))
+
+    def put_base(change, runs):
+        control = columns(c_mid, [(c + 1, n) for c, n in runs]).astype(F32)
+        value = columns(mid, runs) + product(tb_ref, (change + control).astype(BF))
+        done = 0
+        for c, n in runs:
+            for w in range(n):
+                base_new[pl.ds(c + w, C, tile_cols), :] = value[:, done * LANE : (done + 1) * LANE]
+                done += 1
+
     inner = []
     left = half_cols - 2
     while left > 0:
         take = min(left, strip_cols)
         inner.append([(near_start + half_cols - 1 - left, take)])
         left -= take
-    for i, runs in enumerate(inner):
-        inner_mid[i, :, : runs[0][1] * LANE] = convolve(2, shifts_c, runs)
-    pack_weights(1)
-
-    await_edges(1, shifts_h, ROW_SIDES)
-    halo = tile_halo(1, 2)
-    inner_start = inward[0] * strip_cols
-    rolled = pltpu.roll(halo, lax.rem(LANE - inner_start, LANE), 1)
-    for i in range(strip_cols + 2):
-        shift(shifts_h, inner_start + i, rolled, i, PACK + i)
-
-    def second(start):
-        own = jnp.concatenate(
-            [base[pl.ds(start + w, C, tile_cols), :] for w in range(strip_cols)], axis=1
-        )
-        mid[:, slot(start, strip_cols)] = convolve(1, shifts_h, [(start, strip_cols)]) + own
-
-    def columns(ref, runs):
-        parts = [ref[:, slot(c, n)] for c, n in runs]
-        return jnp.concatenate(parts, axis=1) if len(parts) > 1 else parts[0]
-
-    def change_of(middle, runs):
-        return middle + product(tc_ref, columns(mid, runs).astype(BF))
-
-    def put_base(change, runs):
-        control = columns(shifts_c.at[1], [(c + 1, n) for c, n in runs]).astype(F32)
-        value = columns(mid, runs) + product(tb_ref, (change + control).astype(BF))
-        done = 0
-        for c, n in runs:
-            for w in range(n):
-                base_new[pl.ds(c + w, C, tile_cols), :] = value[:, done * LANE : (done + 1) * LANE]
-                done += 1
-
-    second(inner_start)
-
-    for copy in t_loads:
-        copy.wait()
-    for q in fars:
-        for w in range(strip_cols):
-            from_strip(q, w).wait_recv()
-        control_edges(q, q).wait_recv()
-    forward_start(1)
-    shift_half(far_start, control_halo(1 + far_base, half, None))
 
     def far_part(j):
         q = inward[j]
@@ -563,15 +578,45 @@
         to_strip(q, r).start()
         far_change[j] = change
 
-    far_part(0)
+    def far_arrive():
+        for q in fars:
+            for copy in from_strip(q):
+                copy.wait_recv()
+            control_edges(q, q).wait_recv()
+        forward_start(1)
+        shift_half(far_start, control_halo(1 + far_base, half, None))
+
+    def near_inner():
+        for i, runs in enumerate(inner):
+            inner_mid[i, :, : runs[0][1] * LANE] = convolve(2, shifts_c, runs)
+
+    def second_first():
+        await_edges(1, shifts_h, ROW_SIDES)
+        rolled = pltpu.roll(tile_halo(1, 2), lax.rem(LANE - inner_start, LANE), 1)
+        for i in range(strip_cols + 2):
+            mend(shifts_h, inner_start + i, rolled, i, PACK + i)
+        second(inner_start)
+
+    @pl.when(r == near_base)
+    def _():
+        far_arrive()
+        second_first()
+        far_part(0)
+        near_inner()
+
+    @pl.when(r != near_base)
+    def _():
+        second_first()
+        near_inner()
+        far_arrive()
+        far_part(0)
 
     await_edges(2, shifts_h, ROW_SIDES + WIDE_SIDES)
-    halo_inner = halo
+    rest_start = far_is_left * (strip_cols + 2)
+    rolled = pltpu.roll(tile_halo(1, 2), lax.rem(LANE - 2 - rest_start, LANE), 1)
+    for i in range(tile_cols - 2 - strip_cols - 2):
+        mend(shifts_h, 2 + rest_start + i, rolled, i, PACK + i)
     halo = tile_halo(2, 6)
-    rest_start = far_is_left * (strip_cols + 2)
-    rolled = pltpu.roll(halo_inner, lax.rem(LANE - 2 - rest_start, LANE), 1)
-    for i in range(tile_cols - 2 - strip_cols - 2):
-        shift(shifts_h, 2 + rest_start + i, rolled, i, PACK + i)
     shift_inner(shifts_h, 1, halo)
     shift_inner(shifts_h, tile_cols, halo)
     shift_ends(shifts_h, halo)
@@ -622,10 +667,28 @@
     for i in range(2):
         forward_sent(i)
     for q in buddies + fars:
-        for w in range(strip_cols):
-            to_tile(q, w).wait_send()
+        for copy in to_tile(q):
+            copy.wait_send()
         control_edges(q, r).wait_send()
         to_strip(q, r).wait_send()
+
+
+def scoped(n_cols, n_rows, *refs):
+    strip_cols = refs[11].shape[2]
+    pl.run_scoped(
+        functools.partial(kernel, n_cols, n_rows, *refs),
+        pltpu.SemaphoreType.DMA((9 + n_rows,)),
+        pltpu.SemaphoreType.DMA((3, 8)),
+        pltpu.SemaphoreType.DMA((3, 8)),
+        pltpu.SemaphoreType.DMA((n_rows, strip_cols, 2)),
+        pltpu.SemaphoreType.DMA((n_rows, strip_cols, 2)),
+        pltpu.SemaphoreType.DMA((n_rows,)),
+        pltpu.SemaphoreType.DMA((n_rows,)),
+        pltpu.SemaphoreType.DMA((2, 2)),
+        pltpu.SemaphoreType.DMA((2, 2)),
+        pltpu.SemaphoreType.DMA((n_rows,)),
+        pltpu.SemaphoreType.DMA((n_rows,)),
+    )
 
 
 def deliver(base_new, ctl, base_out, control_out, sem):
@@ -653,12 +716,12 @@
         tall = -(-C // LANE) * LANE
         area = tile_cols * LANE
         half = n_rows // 2
-        held = pltpu.VMEM((3, C, area + 2 * LANE), BF)
+        held = pltpu.VMEM((C, area + 2 * LANE), BF)
         inner = max(1, -(-(half * strip_cols - 2) // strip_cols))
         hbm = pl.BlockSpec(memory_space=pltpu.HBM)
         vmem = pl.BlockSpec(memory_space=pltpu.VMEM)
         base_new, ctl = pl.pallas_call(
-            functools.partial(kernel, n_cols, n_rows),
+            functools.partial(scoped, n_cols, n_rows),
             out_shape=(
                 pltpu.VMEM((C * tile_cols, LANE), F32),
                 pltpu.VMEM((n_rows, C, strip_cols, LANE), F32),
@@ -669,9 +732,7 @@
                 pltpu.VMEM((C * tile_cols, LANE), F32),
                 pltpu.VMEM((3,) + k1.shape, BF),
                 pltpu.VMEM((3, C, 9 * C), BF),
-                held,
-                held,
-                held,
+                *[held] * 9,
                 pltpu.VMEM((C,), F32),
                 pltpu.VMEM((C,), F32),
                 pltpu.VMEM((C,), F32),
@@ -688,17 +749,6 @@
                 pltpu.VMEM((half, C, wide), F32),
                 pltpu.VMEM((n_rows, C, wide), BF),
                 pltpu.VMEM((n_rows, C, wide), BF),
-                pltpu.SemaphoreType.DMA((9 + n_rows,)),
-                pltpu.SemaphoreType.DMA((3, 8)),
-                pltpu.SemaphoreType.DMA((3, 8)),
-                pltpu.SemaphoreType.DMA((n_rows, strip_cols)),
-                pltpu.SemaphoreType.DMA((n_rows, strip_cols)),
-                pltpu.SemaphoreType.DMA((n_rows,)),
-                pltpu.SemaphoreType.DMA((n_rows,)),
-                pltpu.SemaphoreType.DMA((2, 2)),
-                pltpu.SemaphoreType.DMA((2, 2)),
-                pltpu.SemaphoreType.DMA((n_rows,)),
-                pltpu.SemaphoreType.DMA((n_rows,)),
             ],
             compiler_params=pltpu.CompilerParams(
                 collective_id=0, has_side_effects=True, vmem_limit_bytes=60 * 1024 * 1024

time: 27.3 us -> 25.4 us (0.930)
  Pallas kernels: 26.5 us -> 24.4 us
    pallas_call x1, Pallas kernels: 25 us -> 22.9 us  [per_device(): pl.pallas_call(functools.partial(scoped, n_cols, n_rows), out_shape=(pltp...]
where the time goes in v3:
time: 25.4 us; the launch traced here: 25.2 us
  Pallas kernels  24.4 us (96%)
  between operations  0.8 us (3%)
    pallas_call x1, Pallas kernels, per_device(): pl.pallas_call(functools.partial(scoped, n_cols, n_rows), out_shape=(pltp...  22.9 us
    pallas_call x1, Pallas kernels, per_device(): pl.pallas_call(deliver, out_shape=(jax.ShapeDtypeStruct(base_new.shape, F...  1.52 us

profile of v3, /device:TPU:0, one launch (start us, length us, event | category | flops | bytes accessed | tf_op | source)
XLA Modules:
  0.0 25.2 jit_solution(10435798689591174523)
XLA Ops:
  0.6 22.9 %shard_map.113 = (f32[2560,128]{1,0:T(8,128)S(1)}, f32[4,320,2,128]{3,2,1,0:T(2,128)S(1)}) custom-call(f32[2560,128]{1,0:T(8,128)} %bitcast.2, f32[320,2,512]{2,1,0:T(2,128)} %refs_1_.1, bf16[9,320,320]{2,1,0:T(8,128)(2,1)} %refs_2_.1, bf16[9,320,320]{2,1,0:T(8,128)(2,1)} %refs_3_.1, bf16[9,320,320]{2,1,0:T(8,128)(2,1)} %refs_4_.1, f32[320]{0:T(512)} %refs_5_.1, ...), custom_call_target="tpu_custom_call" | custom-call | tf_op jit(solution)/shard_map/pallas_call | solution.py:723
  23.5 1.5 %shard_map.114 = (f32[2560,128]{1,0:T(8,128)}, f32[320,2,512]{2,1,0:T(2,128)}) custom-call(f32[2560,128]{1,0:T(8,128)S(1)} %get-tuple-element.6.base_new, f32[4,320,2,128]{3,2,1,0:T(2,128)S(1)} %get-tuple-element.7.ctl), custom_call_target="tpu_custom_call" | custom-call | tf_op jit(solution)/shard_map/pallas_call | solution.py:757

commit v4 on v3

--- a/solution.py
+++ b/solution.py
@@ -14,7 +14,7 @@
 PACK = 16
 SIDES = ((-1, 0), (1, 0), (0, -1), (0, 1), (-1, -1), (1, -1), (-1, 1), (1, 1))
 ROW_SIDES = ((0, 1), (0, -1))
-WIDE_SIDES = tuple(side for side in SIDES if side[0])
+WIDE_SIDES = tuple(side for side in SIDES if side[0] and side[1]) + ((-1, 0), (1, 0))
 TAPS = (1, 4, 7, 0, 3, 6, 2, 5, 8)
 NT = (((1,), (1,)), ((), ()))
 
@@ -104,7 +104,8 @@
     near_start = near_base * strip_cols
     far_start = far_base * strip_cols
     buddies = [near_base + lax.rem(r - near_base + o, half) for o in range(1, half)]
-    fars = [far_base + j for j in range(half)]
+    fars = [far_base + j + (1 - far_is_left) * (half - 1 - 2 * j) for j in range(half)]
+    leads = r == near_base + (half - 1) * far_is_left
     inward = [far_base + j + far_is_left * (half - 1 - 2 * j) for j in range(half)]
 
     def load(i, src, dst):
@@ -112,11 +113,14 @@
         copy.start()
         return copy
 
-    base_load = load(0, base_hbm, base)
+    base_loads = []
+    for i, (low, count) in enumerate(((0, middle), (middle, C - middle))):
+        rows = pl.ds(low * tile_cols, count * tile_cols)
+        base_loads.append((low, count, load(i, base_hbm.at[rows, :], base.at[rows, :])))
     ctl_loads = [
-        load(1 + q, control_hbm.at[:, :, pl.ds(q * LANE, LANE)], ctl.at[q]) for q in range(n_rows)
+        load(2 + q, control_hbm.at[:, :, pl.ds(q * LANE, LANE)], ctl.at[q]) for q in range(n_rows)
     ]
-    more = 1 + n_rows
+    more = 2 + n_rows
     weight_loads = [load(more, k1_hbm, raw.at[0])]
     row_loads = [
         load(more + 3 + i, src, dst)
@@ -309,9 +313,12 @@
         count = sum(n for _, n in runs)
         return silu(total + jnp.concatenate([biases[i]] * count, axis=1))
 
-    base_load.wait()
-    for w in range(tile_cols):
-        b_mid[:, slot(w + 1)] = base[pl.ds(w, C, tile_cols), :].astype(BF)
+    for low, count, copy in base_loads:
+        copy.wait()
+        for w in range(tile_cols):
+            b_mid[low : low + count, slot(w + 1)] = base[
+                pl.ds(low * tile_cols + w, count, tile_cols), :
+            ].astype(BF)
     edge_out[0] = pad_rows(
         lax.dot_general(
             edge_picker(0, tile_cols),
@@ -355,7 +362,7 @@
 
     def late_sends(step):
         if half > 1:
-            for copy in to_tile(fars[-1])[step : 1 if step == 0 else None]:
+            for copy in to_tile(fars[-1])[step * strip_cols : (step + 1) * strip_cols]:
                 copy.start()
 
     def control_edges(q, to):
@@ -597,14 +604,14 @@
             mend(shifts_h, inner_start + i, rolled, i, PACK + i)
         second(inner_start)
 
-    @pl.when(r == near_base)
+    @pl.when(leads)
     def _():
         far_arrive()
         second_first()
         far_part(0)
         near_inner()
 
-    @pl.when(r != near_base)
+    @pl.when(jnp.logical_not(leads))
     def _():
         second_first()
         near_inner()
@@ -677,7 +684,7 @@
     strip_cols = refs[11].shape[2]
     pl.run_scoped(
         functools.partial(kernel, n_cols, n_rows, *refs),
-        pltpu.SemaphoreType.DMA((9 + n_rows,)),
+        pltpu.SemaphoreType.DMA((10 + n_rows,)),
         pltpu.SemaphoreType.DMA((3, 8)),
         pltpu.SemaphoreType.DMA((3, 8)),
         pltpu.SemaphoreType.DMA((n_rows, strip_cols, 2)),
@@ -691,19 +698,24 @@
     )
 
 
-def deliver(base_new, ctl, base_out, control_out, sem):
-    n_rows = ctl.shape[0]
-    copies = [pltpu.make_async_copy(base_new, base_out, sem.at[n_rows])]
-    for q in range(n_rows):
-        copies.append(
-            pltpu.make_async_copy(
-                ctl.at[q], control_out.at[:, :, pl.ds(q * LANE, LANE)], sem.at[q]
-            )
-        )
-    for copy in copies:
-        copy.start()
-    for copy in copies:
-        copy.wait()
+def deliver(base_new, ctl, base_out, control_out):
+    def body(sem):
+        n_rows = ctl.shape[0]
+        step = base_new.shape[0] // n_rows
+        copies = []
+        for q in range(n_rows):
+            rows = pl.ds(q * step, step)
+            copies.append((base_new.at[rows, :], base_out.at[rows, :]))
+            copies.append((ctl.at[q], control_out.at[:, :, pl.ds(q * LANE, LANE)]))
+        copies = [
+            pltpu.make_async_copy(src, dst, sem.at[i]) for i, (src, dst) in enumerate(copies)
+        ]
+        for copy in copies:
+            copy.start()
+        for copy in copies:
+            copy.wait()
+
+    pl.run_scoped(body, pltpu.SemaphoreType.DMA((2 * ctl.shape[0],)))
 
 
 def solution(mesh):
@@ -762,7 +774,6 @@
             ),
             in_specs=[vmem] * 2,
             out_specs=(hbm, hbm),
-            scratch_shapes=[pltpu.SemaphoreType.DMA((n_rows + 1,))],
             compiler_params=pltpu.CompilerParams(vmem_limit_bytes=1024 * 1024),
         )(base_new, ctl)
         return base_out.reshape(base.shape), control_out

time: 25.4 us -> 24.9 us (0.980)
  Pallas kernels: 24.4 us -> 24.1 us
where the time goes in v4:
time: 24.9 us; the launch traced here: 24.8 us
  Pallas kernels  24.1 us (97%)
  between operations  0.64 us (3%)
    pallas_call x1, Pallas kernels, per_device(): pl.pallas_call(functools.partial(scoped, n_cols, n_rows), out_shape=(pltp...  22.6 us
    pallas_call x1, Pallas kernels, per_device(): pl.pallas_call(deliver, out_shape=(jax.ShapeDtypeStruct(base_new.shape, F...  1.48 us

profile of v4, /device:TPU:0, one launch (start us, length us, event | category | flops | bytes accessed | tf_op | source)
XLA Modules:
  0.0 24.8 jit_solution(17545699881877021880)
XLA Ops:
  0.6 22.6 %shard_map.113 = (f32[2560,128]{1,0:T(8,128)S(1)}, f32[4,320,2,128]{3,2,1,0:T(2,128)S(1)}) custom-call(f32[2560,128]{1,0:T(8,128)} %bitcast.2, f32[320,2,512]{2,1,0:T(2,128)} %refs_1_.1, bf16[9,320,320]{2,1,0:T(8,128)(2,1)} %refs_2_.1, bf16[9,320,320]{2,1,0:T(8,128)(2,1)} %refs_3_.1, bf16[9,320,320]{2,1,0:T(8,128)(2,1)} %refs_4_.1, f32[320]{0:T(512)} %refs_5_.1, ...), custom_call_target="tpu_custom_call" | custom-call | tf_op jit(solution)/shard_map/pallas_call | solution.py:735
  23.3 1.5 %shard_map.114 = (f32[2560,128]{1,0:T(8,128)}, f32[320,2,512]{2,1,0:T(2,128)}) custom-call(f32[2560,128]{1,0:T(8,128)S(1)} %get-tuple-element.6.base_new, f32[4,320,2,128]{3,2,1,0:T(2,128)S(1)} %get-tuple-element.7.ctl), custom_call_target="tpu_custom_call" | custom-call | tf_op jit(solution)/shard_map/pallas_call | solution.py:769
